TPU v7x, 32 devices: a whole 2x2x4 slice. The times are simulated.
32 devices in a mesh: row: 4 (over y, core), col: 8 (over z, x).
Axes of the slice: x: 2, y: 2, z: 4, core: 2. Of those that a mesh axis runs over, the one named last changes fastest.
Arguments:
- nodes: bfloat16 [256, 256, 128], P('row', 'col'), may hold values from -6 to 6
- edges: bfloat16 [4, 8, 16, 1024, 128], P('row', 'col'), may hold values from -2000 to 2000
- senders: int32 [4, 8, 16, 1024], P('row', 'col'), may hold values from 0 to 203, as said below
- receivers: int32 [4, 8, 16, 1024], P('row', 'col'), may hold values from 0 to 127, as said below
- counts: int32 [4, 8, 16], P('row', 'col'), may hold values from 512 to 1024, as said below
- w_edge_in: bfloat16 [384, 128], replicated, may hold values from -0.3125 to 0.3125
- w_edge_hid: bfloat16 [128, 128], replicated, may hold values from -0.5 to 0.5
- w_edge_out: bfloat16 [128, 128], replicated, may hold values from -0.5 to 0.5
- edge_bias: float32 [3, 128], replicated, may hold values from -3 to 3
- edge_gain: float32 [128], replicated, may hold values from 0.25 to 1.75
- edge_shift: float32 [128], replicated, may hold values from -3 to 3
- w_node_in: bfloat16 [256, 128], replicated, may hold values from -0.375 to 0.375
- w_node_hid: bfloat16 [128, 128], replicated, may hold values from -0.5 to 0.5
- w_node_out: bfloat16 [128, 128], replicated, may hold values from -0.5 to 0.5
- node_bias: float32 [3, 128], replicated, may hold values from -3 to 3
- node_gain: float32 [128], replicated, may hold values from 0.25 to 1.75
- node_shift: float32 [128], replicated, may hold values from -3 to 3
Outputs:
- new_nodes: bfloat16 [256, 256, 128], P('row', 'col')
- new_edges: bfloat16 [4, 8, 16, 1024, 128], P('row', 'col')
Inputs may be any that keep to these rules, and one draw needn't show every extreme that they name: `senders`: the sender of slot k of band b is numbered in the window of node rows b * 4 - 1 to b * 4 + 4 and node columns -1 to 32 of its tile, row by row over 32 + 2 columns; it is one of the eight nodes around the receiver and lies inside the mesh. `receivers`: receivers are numbered row by row over the 4 x 32 nodes of the slot's band. Slots 0 to counts - 1 of a band hold edges, the others are empty; some band of every draw is full.
All inputs are finite; a program needn't handle non-finite values.
Results may differ from a plain program's by a relative error of at most 0.009.
Values may be sent and summed in bfloat16 or wider, within the bound.
A program may use at most 64 MiB of HBM per device.

v0:
```python
import jax
import jax.numpy as jnp
from jax import lax
from jax.sharding import PartitionSpec as P


def extended(value, sides, width):
    for axis, dim in sides:
        devices, length = (lax.axis_size(axis), value.shape[dim])
        up = [(i, (i + 1) % devices) for i in range(devices - 1)]
        down = [(j, i) for i, j in up]
        last = lax.slice_in_dim(value, length - width, length, axis=dim)
        first = lax.slice_in_dim(value, 0, width, axis=dim)
        before = lax.ppermute(last, axis, up)
        after = lax.ppermute(first, axis, down)
        value = jnp.concatenate([before, value, after], axis=dim)
    return value


def layer_norm(values):
    centred = values - jnp.mean(values, axis=-1, keepdims=True)
    spread = jnp.mean(centred * centred, axis=-1, keepdims=True)
    return centred * lax.rsqrt(spread + 1e-05)


def per_device(
    nodes,
    edges,
    senders,
    receivers,
    counts,
    w_edge_in,
    w_edge_hid,
    w_edge_out,
    edge_bias,
    edge_gain,
    edge_shift,
    w_node_in,
    w_node_hid,
    w_node_out,
    node_bias,
    node_gain,
    node_shift,
):
    rows_tile, cols_tile, latent = nodes.shape
    num_bands = edges.shape[2]
    slot_count = edges.shape[3]
    band_rows = rows_tile // num_bands
    tile_edges = edges[0, 0]
    tile_send = senders[0, 0]
    tile_recv = receivers[0, 0]
    tile_counts = counts[0, 0]
    live_mask = (
        lax.broadcasted_iota(jnp.int32, (num_bands, slot_count), 1) < tile_counts[:, None]
    ).astype(jnp.float32)
    local_count = jnp.sum(tile_counts).astype(jnp.float32)
    values = tile_edges.astype(jnp.float32)
    weighted = values * live_mask[..., None]
    local_sum = jnp.sum(weighted, axis=(0, 1))
    local_power = jnp.sum(weighted * values, axis=(0, 1))
    row_count, row_sum, row_power = lax.psum((local_count, local_sum, local_power), "col")
    edge_total, summed, power = lax.psum((row_count, row_sum, row_power), "row")
    edge_mean = summed / edge_total
    edge_var = power / edge_total - edge_mean * edge_mean
    inv_spread = lax.rsqrt(edge_var + 1e-05)
    padded = extended(nodes, (("row", 0), ("col", 1)), 1)
    window_rows = band_rows + 2
    send_columns = lax.broadcasted_iota(jnp.int32, (1, window_rows * (cols_tile + 2)), 1)
    recv_columns = lax.broadcasted_iota(jnp.int32, (1, band_rows * cols_tile), 1)

    def band_step(inputs):
        band_index, edge_block, send_index, recv_index, band_live = inputs
        start_row = band_index * band_rows
        window = lax.dynamic_slice_in_dim(padded, start_row, window_rows, 0).reshape(-1, latent)
        own_nodes = lax.dynamic_slice_in_dim(nodes, start_row, band_rows, 0).reshape(-1, latent)
        pick_send = (send_index[:, None] == send_columns).astype(jnp.bfloat16)
        pick_recv = (recv_index[:, None] == recv_columns).astype(jnp.bfloat16)
        sender_lat = jnp.dot(pick_send, window, preferred_element_type=jnp.float32).astype(
            jnp.bfloat16
        )
        receiver_lat = jnp.dot(pick_recv, own_nodes, preferred_element_type=jnp.float32).astype(
            jnp.bfloat16
        )
        normed = ((edge_block.astype(jnp.float32) - edge_mean) * inv_spread).astype(jnp.bfloat16)
        joined = jnp.concatenate([normed, sender_lat, receiver_lat], axis=1)
        hidden_one = jax.nn.relu(
            jnp.dot(joined, w_edge_in, preferred_element_type=jnp.float32) + edge_bias[0]
        ).astype(jnp.bfloat16)
        hidden_two = jax.nn.relu(
            jnp.dot(hidden_one, w_edge_hid, preferred_element_type=jnp.float32) + edge_bias[1]
        ).astype(jnp.bfloat16)
        message = jnp.dot(hidden_two, w_edge_out, preferred_element_type=jnp.float32) + edge_bias[2]
        fresh = (
            band_live[:, None]
            * (normed.astype(jnp.float32) + layer_norm(message) * edge_gain + edge_shift)
        ).astype(jnp.bfloat16)
        summed_band = lax.dot_general(
            pick_recv, fresh, (((0,), (0,)), ((), ())), preferred_element_type=jnp.float32
        )
        return (fresh, summed_band)

    band_ids = jnp.arange(num_bands, dtype=jnp.int32)
    fresh_edges, band_sums = lax.map(
        band_step, (band_ids, tile_edges, tile_send, tile_recv, live_mask)
    )
    gathered = band_sums.reshape(rows_tile * cols_tile, latent).astype(jnp.bfloat16)
    own_flat = nodes.reshape(rows_tile * cols_tile, latent)
    node_input = jnp.concatenate([own_flat, gathered], axis=1)
    node_one = jax.nn.relu(
        jnp.dot(node_input, w_node_in, preferred_element_type=jnp.float32) + node_bias[0]
    ).astype(jnp.bfloat16)
    node_two = jax.nn.relu(
        jnp.dot(node_one, w_node_hid, preferred_element_type=jnp.float32) + node_bias[1]
    ).astype(jnp.bfloat16)
    node_message = jnp.dot(node_two, w_node_out, preferred_element_type=jnp.float32) + node_bias[2]
    updated = (
        own_flat.astype(jnp.float32) + layer_norm(node_message) * node_gain + node_shift
    ).astype(jnp.bfloat16)
    return (updated.reshape(rows_tile, cols_tile, latent), fresh_edges[None, None])


def solution(mesh):
    in_specs = (
        P("row", "col", None),
        P("row", "col", None, None, None),
        P("row", "col", None, None),
        P("row", "col", None, None),
        P("row", "col", None),
        P(),
        P(),
        P(),
        P(),
        P(),
        P(),
        P(),
        P(),
        P(),
        P(),
        P(),
        P(),
    )
    out_specs = (P("row", "col", None), P("row", "col", None, None, None))
    return jax.shard_map(
        per_device, mesh=mesh, in_specs=in_specs, out_specs=out_specs, check_vma=False
    )
```

profile of v0, /device:TPU:0, one launch (start us, length us, event | category | flops | bytes accessed | tf_op | source)
XLA Modules:
  0.0 182.3 jit_solution(4273616655365461686)
XLA Ops:
  1.4 1.3 collective-permute-start.1
  2.7 3.0 %collective-permute-start = (bf16[1,32,128]{2,1,0:T(8,128)(2,1)S(1)}, bf16[1,32,128]{2,1,0:T(8,128)(2,1)S(1)}, u32[]{:S(2)}, u32[]{:S(2)}) collective-permute-start(bf16[1,32,128]{2,1,0:T(8,128)(2,1)S(1)} %get-tuple-element.202), channel_id=1, source_target_pairs={{0,8},{8,16},{16,24},{1,9},{9,17},{17,25},{2,10},{10,18},{18,26},{... | collective-permute-start | bytes 24584 | tf_op jit(solution)/shard_map/ppermute | solution.py:14
  6.5 6.4 %copy.19 = bf16[1,1,16,1024,128]{3,4,2,1,0:T(8,128)(2,1)} copy(bf16[1,1,16,1024,128]{4,3,2,1,0:T(8,128)(2,1)} %param.20) | data formatting | bytes 8388608 | tf_op args[1]
  12.9 5.1 %fusion.31 = (f32[128]{0:T(128)S(1)}, f32[128]{0:T(128)S(1)}) fusion(f32[16,1024]{1,0:T(8,128)S(1)} %fusion.44, bf16[1,1,16,1024,128]{3,4,2,1,0:T(8,128)(2,1)} %copy.19), kind=kLoop, calls=%fused_computation.46 | loop fusion | flops 10485504 | bytes 4260864 | tf_op jit(solution)/shard_map/reduce_sum | solution.py:60
  19.3 23.6 %all-reduce = (f32[128]{0:T(128)S(1)}, f32[]{:T(128)}, f32[128]{0:T(128)S(1)}) all-reduce(f32[128]{0:T(128)S(1)} %get-tuple-element.147, f32[]{:T(128)S(6)} %convert_element_type.63, f32[128]{0:T(128)S(1)} %get-tuple-element.146), channel_id=1, replica_groups=mesh['row'=4,'col'=8] {'col'}, use_global_device_ids=true, to_apply=%region_1.0 | all-reduce | flops 257 | bytes 2056 | tf_op jit(solution)/shard_map/psum | solution.py:61
  43.0 6.3 %all-reduce.1 = (f32[128]{0:T(128)S(1)}, f32[]{:T(128)}, f32[128]{0:T(128)S(1)}) all-reduce(f32[128]{0:T(128)S(1)} %get-tuple-element.184, f32[]{:T(128)} %get-tuple-element.185, f32[128]{0:T(128)S(1)} %get-tuple-element.186), channel_id=1, replica_groups=mesh['row'=4,'col'=8] {'row'}, use_global_device_ids=true, to_apply=%region_2.0 | all-reduce | flops 257 | bytes 2056 | tf_op jit(solution)/shard_map/psum | solution.py:62
  49.4 1.3 collective-permute-start.2
  50.7 1.3 collective-permute-start.3
  52.7 3.8 %collective-permute-done.3 = bf16[66,1,128]{2,1,0:T(2,128)(2,1)S(1)} collective-permute-done((bf16[66,1,128]{2,1,0:T(2,128)(2,1)S(1)}, bf16[66,1,128]{2,1,0:T(2,128)(2,1)S(1)}, u32[]{:S(2)}, u32[]{:S(2)}) %collective-permute-start.3) | collective-permute-done | bytes 16928 | tf_op jit(solution)/shard_map/ppermute | solution.py:15
  57.0 121.9 %while.13 = (s32[]{:T(128)}, bf16[16,1024,128]{2,1,0:T(8,128)(2,1)}, bf16[16,128,128]{2,1,0:T(8,128)(2,1)S(1)}, f32[16,1024]{1,0:T(8,128)S(1)}, bf16[16,1024,128...) while((s32[]{:T(128)}, ...), condition=%wide.region_12.13_spmd.clone, body=%wide.region_9.12_spmd.clone.sunk | while | flops 295121920 | bytes 6441800 | solution.py:103
  62.1 1.2 multiply_convert_fusion.2
  69.7 1.2 multiply_convert_fusion.2
  77.3 1.2 multiply_convert_fusion.2
  84.9 1.2 multiply_convert_fusion.2
  92.5 1.2 multiply_convert_fusion.2
  100.1 1.2 multiply_convert_fusion.2
  107.8 1.2 multiply_convert_fusion.2
  115.4 1.2 multiply_convert_fusion.2
  123.0 1.2 multiply_convert_fusion.2
  130.6 1.2 multiply_convert_fusion.2
  138.2 1.2 multiply_convert_fusion.2
  145.8 1.2 multiply_convert_fusion.2
  153.4 1.2 multiply_convert_fusion.2
  180.8 1.5 add_convert_fusion
  (340 shorter events, 100.6 us)
Async XLA Ops:
  0.6 178.2 %copy-start = (bf16[256,128]{1,0:T(8,128)(2,1)S(1)}, bf16[256,128]{1,0:T(8,128)(2,1)}, u32[]{:S(2)}) copy-start(bf16[256,128]{1,0:T(8,128)(2,1)} %param.30) | copy-start | bytes 196612
  1.4 47.9 %collective-permute-start.1 = (bf16[1,32,128]{2,1,0:T(8,128)(2,1)S(1)}, bf16[1,32,128]{2,1,0:T(8,128)(2,1)S(1)}, u32[]{:S(2)}, u32[]{:S(2)}) collective-permute-start(bf16[1,32,128]{2,1,0:T(8,128)(2,1)S(1)} %get-tuple-element.201), channel_id=1, source_target_pairs={{8,0},{16,8},{24,16},{9,1},{17,9},{25,17},{10,2},{18,10},{26,18},{... | collective-permute-start | bytes 24584 | tf_op jit(solution)/shard_map/ppermute | solution.py:15
  2.7 46.6 %collective-permute-start = (bf16[1,32,128]{2,1,0:T(8,128)(2,1)S(1)}, bf16[1,32,128]{2,1,0:T(8,128)(2,1)S(1)}, u32[]{:S(2)}, u32[]{:S(2)}) collective-permute-start(bf16[1,32,128]{2,1,0:T(8,128)(2,1)S(1)} %get-tuple-element.202), channel_id=1, source_target_pairs={{0,8},{8,16},{16,24},{1,9},{9,17},{17,25},{2,10},{10,18},{18,26},{... | collective-permute-start | bytes 24584 | tf_op jit(solution)/shard_map/ppermute | solution.py:14
  12.8 5.2 %copy-start.7 = (f32[3,128]{1,0:T(4,128)S(1)}, f32[3,128]{1,0:T(4,128)}, u32[]{:S(2)}) copy-start(f32[3,128]{1,0:T(4,128)} %param.33) | copy-start | bytes 4612
  12.8 5.2 %copy-start.8 = (s32[1,1,16]{2,1,0:T(1,128)S(1)}, s32[1,1,16]{2,1,0:T(1,128)}, u32[]{:S(2)}) copy-start(s32[1,1,16]{2,1,0:T(1,128)} %param.23) | copy-start | bytes 196
  12.9 36.4 %copy-start.1 = (bf16[64,32,128]{2,1,0:T(8,128)(2,1)S(1)}, bf16[64,32,128]{2,1,0:T(8,128)(2,1)}, u32[]{:S(2)}) copy-start(bf16[64,32,128]{2,1,0:T(8,128)(2,1)} %param.19) | copy-start | bytes 1572868
  12.9 44.0 %copy-start.2 = (bf16[128,128]{1,0:T(8,128)(2,1)S(1)}, bf16[128,128]{1,0:T(8,128)(2,1)}, u32[]{:S(2)}) copy-start(bf16[128,128]{1,0:T(8,128)(2,1)} %param.26) | copy-start | bytes 98308
  12.9 44.0 %copy-start.4 = (f32[3,128]{1,0:T(4,128)S(1)}, f32[3,128]{1,0:T(4,128)}, u32[]{:S(2)}) copy-start(f32[3,128]{1,0:T(4,128)} %param.27) | copy-start | bytes 4612
  12.9 44.0 %copy-start.5 = (f32[128]{0:T(128)S(1)}, f32[128]{0:T(128)}, u32[]{:S(2)}) copy-start(f32[128]{0:T(128)} %param.28) | copy-start | bytes 1540
  12.9 44.0 %copy-start.6 = (f32[128]{0:T(128)S(1)}, f32[128]{0:T(128)}, u32[]{:S(2)}) copy-start(f32[128]{0:T(128)} %param.29) | copy-start | bytes 1540
  12.9 44.0 %copy-start.11 = (bf16[384,128]{1,0:T(8,128)(2,1)S(1)}, bf16[384,128]{1,0:T(8,128)(2,1)}, u32[]{:S(2)}) copy-start(bf16[384,128]{1,0:T(8,128)(2,1)} %param.24) | copy-start | bytes 294916
  12.9 44.0 %copy-start.12 = (bf16[128,128]{1,0:T(8,128)(2,1)S(1)}, bf16[128,128]{1,0:T(8,128)(2,1)}, u32[]{:S(2)}) copy-start(bf16[128,128]{1,0:T(8,128)(2,1)} %param.25) | copy-start | bytes 98308
  49.4 3.3 %collective-permute-start.2 = (bf16[66,1,128]{2,1,0:T(2,128)(2,1)S(1)}, bf16[66,1,128]{2,1,0:T(2,128)(2,1)S(1)}, u32[]{:S(2)}, u32[]{:S(2)}) collective-permute-start(bf16[66,1,128]{2,1,0:T(2,128)(2,1)S(1)} %get-tuple-element.199), channel_id=1, source_target_pairs={{0,1},{1,2},{2,3},{3,4},{4,5},{5,6},{6,7},{8,9},{9,10},{10,11},{11... | collective-permute-start | bytes 50696 | tf_op jit(solution)/shard_map/ppermute | solution.py:14
  50.7 5.8 %collective-permute-start.3 = (bf16[66,1,128]{2,1,0:T(2,128)(2,1)S(1)}, bf16[66,1,128]{2,1,0:T(2,128)(2,1)S(1)}, u32[]{:S(2)}, u32[]{:S(2)}) collective-permute-start(bf16[66,1,128]{2,1,0:T(2,128)(2,1)S(1)} %get-tuple-element.200), channel_id=1, source_target_pairs={{1,0},{2,1},{3,2},{4,3},{5,4},{6,5},{7,6},{9,8},{10,9},{11,10},{12... | collective-permute-start | bytes 50696 | tf_op jit(solution)/shard_map/ppermute | solution.py:15
  56.9 121.9 %copy-start.13 = (bf16[128,128]{1,0:T(8,128)(2,1)S(1)}, bf16[128,128]{1,0:T(8,128)(2,1)}, u32[]{:S(2)}) copy-start(bf16[128,128]{1,0:T(8,128)(2,1)} %param.31) | copy-start | bytes 98308
  57.0 122.7 %copy-start.3 = (bf16[128,128]{1,0:T(8,128)(2,1)S(1)}, bf16[128,128]{1,0:T(8,128)(2,1)}, u32[]{:S(2)}) copy-start(bf16[128,128]{1,0:T(8,128)(2,1)} %param.32) | copy-start | bytes 98308
  178.8 2.0 %copy-start.9 = (f32[128]{0:T(128)S(1)}, f32[128]{0:T(128)}, u32[]{:S(2)}) copy-start(f32[128]{0:T(128)} %param.35) | copy-start | bytes 1540
  178.8 2.0 %copy-start.10 = (f32[128]{0:T(128)S(1)}, f32[128]{0:T(128)}, u32[]{:S(2)}) copy-start(f32[128]{0:T(128)} %param.34) | copy-start | bytes 1540
where the time goes:
time: 185 us; the launch traced here: 182 us
  other arithmetic  48.6 us (26%)
  local copies, waits for them, and re-layouts  44.6 us (24%)
  matrix products  35.9 us (19%)
  blocking collectives  29.9 us (16%)
  loops' own time  11 us (6%)
  starting transfers between devices  6.89 us (4%)
  waiting for transfers between devices  3.84 us (2%)
    psum x1, blocking collectives, per_device(): lax.psum((local_count, local_sum, local_power), 'col')  23.6 us
    dynamic_slice x48, local copies, waits for them, and re-layouts, per_device(): lax.map(band_step, (band_ids, tile_edges, tile_send, tile_recv, live_mask))  22.1 us
    convert_element_type x16, other arithmetic, band_step(): fresh = (band_live[:, None] * (normed.astype(jnp.float32) + layer_norm(me...  19.2 us
    convert_element_type x16, other arithmetic, band_step(): ((edge_block.astype(jnp.float32) - edge_mean) * inv_spread).astype(jnp.bf...  18.6 us
    dynamic_update_slice x32, local copies, waits for them, and re-layouts, per_device(): lax.map(band_step, (band_ids, tile_edges, tile_send, tile_recv, live_mask))  14.3 us
    another operation x1, loops' own time, per_device(): lax.map(band_step, (band_ids, tile_edges, tile_send, tile_recv, live_mask))  11 us
    dot_general x16, matrix products, band_step(): jnp.dot(hidden_one, w_edge_hid, preferred_element_type=jnp.float32)  9.18 us
    dot_general x16, matrix products, band_step(): jnp.dot(pick_send, window, preferred_element_type=jnp.float32)  7.48 us
  transfers between devices with their start and end apart: 4, of which 1 were waited for; matrix products, arithmetic and copies ran while one was open for 7% of the time, Pallas kernels for 0%

commit v1 on v0

v1 whole, which is shorter than its diff:
```python
import functools

import jax
import jax.numpy as jnp
from jax import lax
from jax.experimental import pallas as pl
from jax.experimental.pallas import tpu as pltpu
from jax.sharding import PartitionSpec as P

MESH = pl.DeviceIdType.MESH
EPS = 1e-05
TAIL = 16
F32 = jnp.float32
BF16 = jnp.bfloat16
VMEM = pl.BlockSpec(memory_space=pltpu.VMEM)
SMEM = pl.BlockSpec(memory_space=pltpu.SMEM)
ANY = pl.BlockSpec(memory_space=pl.ANY)


def dot(a, b):
    return jnp.dot(a, b, preferred_element_type=F32)


def stats_kernel(bands_step, counts, edges, stats, acc_sum, acc_sq, shift):
    step = pl.program_id(0)
    slots, latent = edges.shape[1:]

    @pl.when(step == 0)
    def _():
        shift[...] = jnp.broadcast_to(edges[0, 0:TAIL, :].astype(F32)[0:1], shift.shape)
        acc_sum[...] = jnp.zeros_like(acc_sum)
        acc_sq[...] = jnp.zeros_like(acc_sq)

    base = shift[0:1, :]
    total, square = acc_sum[...], acc_sq[...]
    for k in range(bands_step):
        count = counts[step * bands_step + k]
        rows = lax.broadcasted_iota(jnp.int32, (slots, latent), 0)
        moved = jnp.where(rows < count, edges[k].astype(F32) - base, 0.0)
        total += jnp.sum(moved.reshape(-1, 8, latent), axis=0)
        square += jnp.sum((moved * moved).reshape(-1, 8, latent), axis=0)
    acc_sum[...] = total
    acc_sq[...] = square

    @pl.when(step == pl.num_programs(0) - 1)
    def _():
        number = counts[0]
        for k in range(1, counts.shape[0]):
            number = number + counts[k]
        number = jnp.full((1, latent), number.astype(F32))
        first = jnp.sum(acc_sum[...], axis=0, keepdims=True)
        second = jnp.sum(acc_sq[...], axis=0, keepdims=True)
        offset = first / number
        stats[0:1, :] = base + offset
        stats[1:2, :] = second - first * offset
        stats[2:3, :] = number
        stats[3:8, :] = jnp.zeros((5, latent), F32)


def combine(tiles):
    number = sum(tile[2:3] for tile in tiles)
    mean = sum(tile[2:3] * tile[0:1] for tile in tiles) / number
    power = sum(tile[1:2] + tile[2:3] * (tile[0:1] - mean) * (tile[0:1] - mean) for tile in tiles)
    return mean, power, number


def exchange_kernel(
    num_rows, num_cols, stats, row_edge, col_edge, norm, halo_row, halo_col,
    first, middle, second, send_sem, recv_sem, stat_send, stat_recv,
):
    r, c = lax.axis_index("row"), lax.axis_index("col")

    def at(dr, dc):
        return (lax.rem(r + dr + num_rows, num_rows), lax.rem(c + dc + num_cols, num_cols))

    near = [(0, k) for k in range(1, num_cols)] + [(k, 0) for k in range(1, num_rows)]
    peers = near + [(1, 1), (1, -1), (-1, 1), (-1, -1)]
    barrier = pltpu.get_barrier_semaphore()
    for dr, dc in peers:
        pl.semaphore_signal(barrier, inc=1, device_id=at(dr, dc), device_id_type=MESH)
    pl.semaphore_wait(barrier, len(peers))

    def send(src, dst, ss, rs, dr, dc):
        copy = pltpu.make_async_remote_copy(
            src_ref=src, dst_ref=dst, send_sem=ss, recv_sem=rs,
            device_id=at(dr, dc), device_id_type=MESH,
        )
        copy.start()
        return copy

    stage = [
        send(stats, first.at[k - 1], stat_send.at[k - 1], stat_recv.at[k - 1], 0, k)
        for k in range(1, num_cols)
    ]
    length = col_edge.shape[1]
    top, low = pl.ds(0, TAIL), pl.ds(length - TAIL, TAIL)
    plan = [
        (col_edge.at[1], halo_col.at[0, pl.ds(TAIL, length)], 0, 1),
        (col_edge.at[0], halo_col.at[1, pl.ds(TAIL, length)], 0, -1),
        (row_edge.at[1], halo_row.at[0], 1, 0),
        (row_edge.at[0], halo_row.at[1], -1, 0),
        (col_edge.at[1, low], halo_col.at[0, top], 1, 1),
        (col_edge.at[1, top], halo_col.at[0, pl.ds(TAIL + length, TAIL)], -1, 1),
        (col_edge.at[0, low], halo_col.at[1, top], 1, -1),
        (col_edge.at[0, top], halo_col.at[1, pl.ds(TAIL + length, TAIL)], -1, -1),
    ]
    halo = [
        send(src, dst, send_sem.at[i], recv_sem.at[i], dr, dc)
        for i, (src, dst, dr, dc) in enumerate(plan)
    ]
    for copy in stage:
        copy.wait()
    mean, power, number = combine([stats[...]] + [first[k] for k in range(num_cols - 1)])
    latent = stats.shape[1]
    middle[...] = jnp.concatenate([mean, power, number, jnp.zeros((5, latent), F32)], axis=0)
    base = num_cols - 1
    stage = [
        send(middle, second.at[k - 1], stat_send.at[base + k - 1], stat_recv.at[base + k - 1], k, 0)
        for k in range(1, num_rows)
    ]
    for copy in stage:
        copy.wait()
    mean, power, number = combine([middle[...]] + [second[k] for k in range(num_rows - 1)])
    spread = lax.rsqrt(power / number + EPS)
    norm[...] = jnp.concatenate([mean, spread, jnp.zeros((6, latent), F32)], axis=0)
    for copy in halo:
        copy.wait()


def twice(w):
    zero = jnp.zeros_like(w)
    return jnp.concatenate(
        [jnp.concatenate([w, zero], axis=1), jnp.concatenate([zero, w], axis=1)], axis=0
    )


def centred(w):
    wide = w.astype(F32)
    return wide - jnp.mean(wide, axis=-1, keepdims=True)


def main_kernel(
    band_rows, cols, counts, edges, send_all, recv_all, nodes, halo_row, halo_col, norm,
    w_in, w_hid, w_out, bias, gain, shift, v_in, v_hid, v_out, n_bias, n_gain, n_shift,
    new_edges, new_nodes,
    proj_send, proj_left, proj_right, proj_recv, mixed, two_hid, two_out, two_mean, gathered,
):
    band = pl.program_id(0)
    slots, latent = edges.shape[1:]
    band_nodes = band_rows * cols
    window_rows = band_rows + 2
    main = window_rows * cols
    table = mixed.shape[0] - band_nodes - latent
    half = slots // 2

    @pl.when(band == 0)
    def _():
        w_send = w_in[latent : 2 * latent, :]
        w_recv = w_in[2 * latent :, :]
        total = nodes.shape[0]
        proj_send[0:cols, :] = dot(halo_row[0], w_send).astype(BF16)
        proj_send[cols : cols + total, :] = dot(nodes[...], w_send).astype(BF16)
        proj_send[cols + total :, :] = dot(halo_row[1], w_send).astype(BF16)
        proj_left[...] = dot(halo_col[0], w_send)
        proj_right[...] = dot(halo_col[1], w_send)
        proj_recv[...] = (dot(nodes[...], w_recv) + bias[0:1, :]).astype(BF16)
        mixed[...] = jnp.zeros_like(mixed)
        mixed[table + band_nodes :, :] = w_in[0:latent, :]
        two_hid[...] = twice(w_hid[...])
        two_out[...] = twice(centred(w_out[...]).astype(BF16))
        two_mean[...] = twice(jnp.full((latent, latent), 1.0 / latent, BF16))

    start = pl.multiple_of(band * band_nodes, band_nodes)
    side = TAIL - 1 + band * band_rows
    mixed[0:main, :] = proj_send[pl.ds(start, main), :]
    mixed[main : main + 16, :] = jnp.concatenate(
        [proj_left[pl.ds(side, 8), :], proj_right[pl.ds(side, 8), :]], axis=0
    ).astype(BF16)
    mixed[table : table + band_nodes, :] = proj_recv[pl.ds(start, band_nodes), :]
    weights = mixed[...]

    send = send_all[pl.ds(band, 1), :]
    recv = recv_all[pl.ds(band, 1), :]
    row = sum((send >= (cols + 2) * k).astype(jnp.int32) for k in range(1, window_rows))
    col = send - (cols + 2) * row
    place = jnp.where(
        col == 0, main + row, jnp.where(col == cols + 1, main + 8 + row, row * cols + col - 1)
    )
    count = counts[band]
    mean, spread = norm[0:1, :], norm[1:2, :]
    bias_hid = jnp.concatenate([bias[1:2, :]] * 2, axis=1)
    bias_msg = bias[2:3, :] - jnp.mean(bias[2:3, :], axis=-1, keepdims=True)
    bias_out = jnp.concatenate([bias_msg] * 2, axis=1)

    def spread_rows(index, lo):
        return jnp.broadcast_to(index[:, lo : lo + 128], (128, 128)).T

    def pick(values, width, offset=0):
        lanes = lax.broadcasted_iota(jnp.int32, (values.shape[0], width), 1) + offset
        return jnp.where(values == lanes, 1.0, 0.0).astype(BF16)

    ones, normed = [], []
    for part in range(2):
        pieces = []
        for lo in range(part * half, (part + 1) * half, 128):
            s, q = spread_rows(place, lo), spread_rows(recv, lo)
            hot = [pick(s, 128, off) for off in range(0, table, 128)]
            hot += [pick(q, 128, off) for off in range(0, band_nodes, 128)]
            pieces.append(jnp.concatenate(hot, axis=1))
        hot = jnp.concatenate(pieces, axis=0)
        block = edges[0, part * half : (part + 1) * half, :].astype(F32)
        value = ((block - mean) * spread).astype(BF16)
        normed.append(value)
        joined = jnp.concatenate([hot, value], axis=1)
        ones.append(jnp.maximum(dot(joined, weights), 0.0).astype(BF16))
    one = jnp.concatenate(ones, axis=1)
    two = jnp.maximum(dot(one, two_hid[...]) + bias_hid, 0.0).astype(BF16)
    message = dot(two, two_out[...]) + bias_out
    power = dot((message * message).astype(BF16), two_mean[...])
    unit = message * lax.rsqrt(power + EPS)
    fresh = []
    for part in range(2):
        rows = lax.broadcasted_iota(jnp.int32, (half, latent), 0) + part * half
        value = normed[part].astype(F32) + unit[:, part * latent : (part + 1) * latent] * gain[...] + shift[...]
        value = jnp.where(rows < count, value, 0.0).astype(BF16)
        new_edges[0, part * half : (part + 1) * half, :] = value
        fresh.append(value)
    fresh = jnp.concatenate(fresh, axis=0)
    places = lax.broadcasted_iota(jnp.int32, (band_nodes, slots), 0)
    pick_recv = jnp.where(places == recv, 1.0, 0.0).astype(BF16)
    gathered[pl.ds(start, band_nodes), :] = dot(pick_recv, fresh).astype(BF16)

    @pl.when(band == pl.num_programs(0) - 1)
    def _():
        own = nodes[...]
        joined = jnp.concatenate([own, gathered[...]], axis=1)
        node_one = jnp.maximum(dot(joined, v_in[...]) + n_bias[0:1, :], 0.0).astype(BF16)
        node_two = jnp.maximum(dot(node_one, v_hid[...]) + n_bias[1:2, :], 0.0).astype(BF16)
        out_bias = n_bias[2:3, :] - jnp.mean(n_bias[2:3, :], axis=-1, keepdims=True)
        note = dot(node_two, centred(v_out[...]).astype(BF16)) + out_bias
        level = dot((note * note).astype(BF16), jnp.full((latent, latent), 1.0 / latent, BF16))
        value = own.astype(F32) + note * lax.rsqrt(level + EPS) * n_gain[...] + n_shift[...]
        new_nodes[...] = value.astype(BF16)


def round_up(value, unit):
    return -(-value // unit) * unit


def per_device(
    nodes, edges, senders, receivers, counts, w_edge_in, w_edge_hid, w_edge_out, edge_bias,
    edge_gain, edge_shift, w_node_in, w_node_hid, w_node_out, node_bias, node_gain, node_shift,
):
    rows, cols, latent = nodes.shape
    bands, slots = edges.shape[2:4]
    band_rows = rows // bands
    num_rows, num_cols = lax.axis_size("row"), lax.axis_size("col")
    tile_edges = edges.reshape(bands, slots, latent)
    tile_send = senders.reshape(bands, slots)
    tile_recv = receivers.reshape(bands, slots)
    tile_counts = counts.reshape(bands)
    flat = nodes.reshape(rows * cols, latent)

    step = 2 if bands % 2 == 0 else 1
    stats = pl.pallas_call(
        functools.partial(stats_kernel, step),
        grid=(bands // step,),
        in_specs=[SMEM, pl.BlockSpec((step, slots, latent), lambda i: (i, 0, 0))],
        out_specs=VMEM,
        out_shape=jax.ShapeDtypeStruct((8, latent), F32),
        scratch_shapes=[pltpu.VMEM((8, latent), F32)] * 3,
        name="stats",
    )(tile_counts, tile_edges)

    row_edge = jnp.stack([nodes[0], nodes[-1]])
    col_edge = jnp.stack([nodes[:, 0], nodes[:, -1]])
    stages = num_cols + num_rows - 2
    norm, halo_row, halo_col = pl.pallas_call(
        functools.partial(exchange_kernel, num_rows, num_cols),
        in_specs=[VMEM] * 3,
        out_specs=[VMEM] * 3,
        out_shape=[
            jax.ShapeDtypeStruct((8, latent), F32),
            jax.ShapeDtypeStruct((2, cols, latent), BF16),
            jax.ShapeDtypeStruct((2, rows + 2 * TAIL, latent), BF16),
        ],
        scratch_shapes=[
            pltpu.VMEM((max(num_cols - 1, 1), 8, latent), F32),
            pltpu.VMEM((8, latent), F32),
            pltpu.VMEM((max(num_rows - 1, 1), 8, latent), F32),
            pltpu.SemaphoreType.DMA((8,)),
            pltpu.SemaphoreType.DMA((8,)),
            pltpu.SemaphoreType.DMA((stages,)),
            pltpu.SemaphoreType.DMA((stages,)),
        ],
        compiler_params=pltpu.CompilerParams(collective_id=0, has_side_effects=True),
        name="exchange",
    )(stats, row_edge, col_edge)

    band_nodes = band_rows * cols
    table = round_up((band_rows + 2) * cols + 16, 128)
    out_edges, out_nodes = pl.pallas_call(
        functools.partial(main_kernel, band_rows, cols),
        grid=(bands,),
        in_specs=[SMEM, pl.BlockSpec((1, slots, latent), lambda i: (i, 0, 0))] + [VMEM] * 18,
        out_specs=[pl.BlockSpec((1, slots, latent), lambda i: (i, 0, 0)), VMEM],
        out_shape=[
            jax.ShapeDtypeStruct((bands, slots, latent), BF16),
            jax.ShapeDtypeStruct((rows * cols, latent), BF16),
        ],
        scratch_shapes=[
            pltpu.VMEM(((rows + 2) * cols, latent), BF16),
            pltpu.VMEM((rows + 2 * TAIL, latent), F32),
            pltpu.VMEM((rows + 2 * TAIL, latent), F32),
            pltpu.VMEM((rows * cols, latent), BF16),
            pltpu.VMEM((table + band_nodes + latent, latent), BF16),
            pltpu.VMEM((2 * latent, 2 * latent), BF16),
            pltpu.VMEM((2 * latent, 2 * latent), BF16),
            pltpu.VMEM((2 * latent, 2 * latent), BF16),
            pltpu.VMEM((rows * cols, latent), BF16),
        ],
        name="processor",
    )(
        tile_counts, tile_edges, tile_send, tile_recv, flat, halo_row, halo_col, norm,
        w_edge_in, w_edge_hid, w_edge_out, edge_bias, edge_gain.reshape(1, latent),
        edge_shift.reshape(1, latent), w_node_in, w_node_hid, w_node_out, node_bias,
        node_gain.reshape(1, latent), node_shift.reshape(1, latent),
    )
    return out_nodes.reshape(rows, cols, latent), out_edges.reshape(edges.shape)


def solution(mesh):
    tile = ("row", "col")
    in_specs = (
        P(*tile, None),
        P(*tile, None, None, None),
        P(*tile, None, None),
        P(*tile, None, None),
        P(*tile, None),
    ) + (P(),) * 12
    out_specs = (P(*tile, None), P(*tile, None, None, None))
    return jax.shard_map(
        per_device, mesh=mesh, in_specs=in_specs, out_specs=out_specs, check_vma=False
    )
```

time: 185 us -> 48 us (0.26); the launches traced: 182 us -> 47.7 us
  other arithmetic: 48.6 us -> 1.23 us
  Pallas kernels: 0 us -> 44 us
  local copies, waits for them, and re-layouts: 44.6 us -> 1.75 us
  matrix products: 35.9 us -> 0 us
  blocking collectives: 29.9 us -> 0 us
  loops' own time: 11 us -> 0 us
  starting transfers between devices: 6.89 us -> 0 us
  waiting for transfers between devices: 3.84 us -> 0 us
    pallas_call x0 -> x3, Pallas kernels: none -> 44 us  [the longest x1 24.1 us: per_device(): pl.pallas_call(functools.partial(main_kernel, band_rows, cols), grid=(ban...]
    convert_element_type x34 -> x0, other arithmetic: 40 us -> none  [the longest x16 19.2 us: band_step(): fresh = (band_live[:, None] * (normed.astype(jnp.float32) + layer_norm(me...]
    dot_general x82 -> x0, matrix products: 35.9 us -> none  [the longest x16 9.18 us: band_step(): jnp.dot(hidden_one, w_edge_hid, preferred_element_type=jnp.float32)]
    psum x2 -> x0, blocking collectives: 29.9 us -> none  [the longest x1 23.6 us: per_device(): lax.psum((local_count, local_sum, local_power), 'col')]
    dynamic_slice x80 -> x0, local copies, waits for them, and re-layouts: 22.5 us -> none  [the longest x48 22.1 us: per_device(): lax.map(band_step, (band_ids, tile_edges, tile_send, tile_recv, live_mask))]
    dynamic_update_slice x32 -> x0, local copies, waits for them, and re-layouts: 14.3 us -> none  [per_device(): lax.map(band_step, (band_ids, tile_edges, tile_send, tile_recv, live_mask))]
    another operation x1 -> x0, loops' own time: 11 us -> none  [per_device(): lax.map(band_step, (band_ids, tile_edges, tile_send, tile_recv, live_mask))]
    reduce_sum x19 -> x0, other arithmetic: 7.49 us -> none  [the longest x1 5.1 us: per_device(): local_power = jnp.sum(weighted * values, axis=(0, 1))]
  transfers between devices with their start and end apart: 4 -> 0, of which waited for: 1 -> 0; matrix products, arithmetic and copies ran while one was open for 7% -> 0% of each run, Pallas kernels for 0% -> 0%
where the time goes in v1:
time: 48 us; the launch traced here: 47.7 us
  Pallas kernels  44 us (92%)
  local copies, waits for them, and re-layouts  1.75 us (4%)
  other arithmetic  1.23 us (3%)
  between operations  0.65 us (1%)
    pallas_call x1, Pallas kernels, per_device(): pl.pallas_call(functools.partial(main_kernel, band_rows, cols), grid=(ban...  24.1 us
    pallas_call x1, Pallas kernels, per_device(): pl.pallas_call(functools.partial(exchange_kernel, num_rows, num_cols), in...  13.3 us
    pallas_call x1, Pallas kernels, per_device(): pl.pallas_call(functools.partial(stats_kernel, step), grid=(bands // step...  6.67 us
    slice x1, local copies, waits for them, and re-layouts, per_device(): col_edge = jnp.stack([nodes[:, 0], nodes[:, -1]])  1.03 us

profile of v1, /device:TPU:0, one launch (start us, length us, event | category | flops | bytes accessed | tf_op | source)
XLA Modules:
  0.0 47.7 jit_solution(5263359030383796850)
XLA Ops:
  0.6 6.7 %stats.1 = f32[8,128]{1,0:T(8,128)} custom-call(s32[16]{0:T(128)} %bitcast.20, bf16[16,1024,128]{2,1,0:T(8,128)(2,1)} %bitcast.15), custom_call_target="tpu_custom_call" | custom-call | tf_op jit(solution)/shard_map/stats/pallas_call | solution.py:265
  7.3 0.7 %fusion.1 = (bf16[1,32,128]{2,1,0:T(8,128)(2,1)S(1)}, bf16[1,32,128]{2,1,0:T(8,128)(2,1)S(1)}) fusion(bf16[64,32,128]{2,1,0:T(8,128)(2,1)} %param.17), kind=kLoop, calls=%fused_computation.5 | loop fusion | bytes 32768 | tf_op jit(solution)/shard_map/slice | solution.py:275
  8.0 0.6 %pad_maximum_fusion.1.row_edge = bf16[2,32,128]{2,1,0:T(8,128)(2,1)} fusion(bf16[1,32,128]{2,1,0:T(8,128)(2,1)S(1)} %get-tuple-element.15, bf16[1,32,128]{2,1,0:T(8,128)(2,1)S(1)} %get-tuple-element.14), kind=kLoop, calls=%fused_computation.1 | loop fusion | flops 8192 | bytes 32768 | tf_op jit(solution)/shard_map/stack | solution.py:275
  8.6 1.0 %fusion = (bf16[64,1,128]{2,1,0:T(2,128)(2,1)S(1)}, bf16[64,1,128]{2,1,0:T(2,128)(2,1)S(1)}) fusion(bf16[64,32,128]{2,1,0:T(8,128)(2,1)} %param.17), kind=kLoop, calls=%fused_computation.4 | loop fusion | bytes 65536 | tf_op jit(solution)/shard_map/slice | solution.py:276
  9.7 0.6 %pad_maximum_fusion.col_edge = bf16[2,64,128]{2,1,0:T(8,128)(2,1)} fusion(bf16[1,64,128]{2,1,0:T(8,128)(2,1)S(1)} %get-tuple-element.16, bf16[1,64,128]{2,1,0:T(8,128)(2,1)S(1)} %get-tuple-element.17), kind=kLoop, calls=%fused_computation | loop fusion | flops 16384 | bytes 65536 | tf_op jit(solution)/shard_map/stack | solution.py:276
  10.3 13.3 %exchange.1 = (f32[8,128]{1,0:T(8,128)}, bf16[2,32,128]{2,1,0:T(8,128)(2,1)}, bf16[2,96,128]{2,1,0:T(8,128)(2,1)}) custom-call(f32[8,128]{1,0:T(8,128)} %stats.1, bf16[2,32,128]{2,1,0:T(8,128)(2,1)} %pad_maximum_fusion.1.row_edge, bf16[2,64,128]{2,1,0:T(8,128)(2,1)} %pad_maximum_fusion.col_edge), custom_call_target="tpu_custom_call" | custom-call | tf_op jit(solution)/shard_map/exchange/pallas_call | solution.py:278
  23.6 24.1 %processor.1 = (bf16[16,1024,128]{2,1,0:T(8,128)(2,1)}, bf16[2048,128]{1,0:T(8,128)(2,1)}) custom-call(s32[16]{0:T(128)} %bitcast.21, bf16[16,1024,128]{2,1,0:T(8,128)(2,1)} %bitcast.16, s32[16,1024]{1,0:T(8,128)} %bitcast.18, s32[16,1024]{1,0:T(8,128)} %bitcast.19, bf16[2048,128]{1,0:T(8,128)(2,1)} %bitcast.17, ...), custom_call_target="tpu_custom_call" | custom-call | tf_op jit(solution)/shard_map/processor/pallas_call | solution.py:302
  (1 shorter events, 0.0 us)

commit v2 on v1

--- a/solution.py
+++ b/solution.py
@@ -21,54 +21,23 @@
     return jnp.dot(a, b, preferred_element_type=F32)
 
 
-def stats_kernel(bands_step, counts, edges, stats, acc_sum, acc_sq, shift):
-    step = pl.program_id(0)
+def combine(tiles, latent):
+    parts = [[tile[:, k * latent : (k + 1) * latent] for k in range(3)] for tile in tiles]
+    number = sum(n for _, _, n in parts)
+    mean = sum(n * m for m, _, n in parts) / number
+    power = sum(p + n * (m - mean) * (m - mean) for m, p, n in parts)
+    return mean, power, number
+
+
+def exchange_kernel(
+    num_rows, num_cols, bands_step, counts, edges, nodes, norm, row_out, col_out,
+    halo_row, halo_col, acc_sum, acc_sq, shift, col_edge, stats, first, middle, second,
+    send_sem, recv_sem, stat_send, stat_recv,
+):
+    step, steps = pl.program_id(0), pl.num_programs(0)
+    r, c = lax.axis_index("row"), lax.axis_index("col")
     slots, latent = edges.shape[1:]
-
-    @pl.when(step == 0)
-    def _():
-        shift[...] = jnp.broadcast_to(edges[0, 0:TAIL, :].astype(F32)[0:1], shift.shape)
-        acc_sum[...] = jnp.zeros_like(acc_sum)
-        acc_sq[...] = jnp.zeros_like(acc_sq)
-
-    base = shift[0:1, :]
-    total, square = acc_sum[...], acc_sq[...]
-    for k in range(bands_step):
-        count = counts[step * bands_step + k]
-        rows = lax.broadcasted_iota(jnp.int32, (slots, latent), 0)
-        moved = jnp.where(rows < count, edges[k].astype(F32) - base, 0.0)
-        total += jnp.sum(moved.reshape(-1, 8, latent), axis=0)
-        square += jnp.sum((moved * moved).reshape(-1, 8, latent), axis=0)
-    acc_sum[...] = total
-    acc_sq[...] = square
-
-    @pl.when(step == pl.num_programs(0) - 1)
-    def _():
-        number = counts[0]
-        for k in range(1, counts.shape[0]):
-            number = number + counts[k]
-        number = jnp.full((1, latent), number.astype(F32))
-        first = jnp.sum(acc_sum[...], axis=0, keepdims=True)
-        second = jnp.sum(acc_sq[...], axis=0, keepdims=True)
-        offset = first / number
-        stats[0:1, :] = base + offset
-        stats[1:2, :] = second - first * offset
-        stats[2:3, :] = number
-        stats[3:8, :] = jnp.zeros((5, latent), F32)
-
-
-def combine(tiles):
-    number = sum(tile[2:3] for tile in tiles)
-    mean = sum(tile[2:3] * tile[0:1] for tile in tiles) / number
-    power = sum(tile[1:2] + tile[2:3] * (tile[0:1] - mean) * (tile[0:1] - mean) for tile in tiles)
-    return mean, power, number
-
-
-def exchange_kernel(
-    num_rows, num_cols, stats, row_edge, col_edge, norm, halo_row, halo_col,
-    first, middle, second, send_sem, recv_sem, stat_send, stat_recv,
-):
-    r, c = lax.axis_index("row"), lax.axis_index("col")
+    length, cols = nodes.shape[0:2]
 
     def at(dr, dc):
         return (lax.rem(r + dr + num_rows, num_rows), lax.rem(c + dc + num_cols, num_cols))
@@ -76,55 +45,106 @@
     near = [(0, k) for k in range(1, num_cols)] + [(k, 0) for k in range(1, num_rows)]
     peers = near + [(1, 1), (1, -1), (-1, 1), (-1, -1)]
     barrier = pltpu.get_barrier_semaphore()
-    for dr, dc in peers:
-        pl.semaphore_signal(barrier, inc=1, device_id=at(dr, dc), device_id_type=MESH)
-    pl.semaphore_wait(barrier, len(peers))
-
-    def send(src, dst, ss, rs, dr, dc):
-        copy = pltpu.make_async_remote_copy(
+
+    def copy_of(src, dst, ss, rs, dr, dc):
+        return pltpu.make_async_remote_copy(
             src_ref=src, dst_ref=dst, send_sem=ss, recv_sem=rs,
             device_id=at(dr, dc), device_id_type=MESH,
         )
-        copy.start()
-        return copy
-
-    stage = [
-        send(stats, first.at[k - 1], stat_send.at[k - 1], stat_recv.at[k - 1], 0, k)
-        for k in range(1, num_cols)
-    ]
-    length = col_edge.shape[1]
+
     top, low = pl.ds(0, TAIL), pl.ds(length - TAIL, TAIL)
     plan = [
         (col_edge.at[1], halo_col.at[0, pl.ds(TAIL, length)], 0, 1),
         (col_edge.at[0], halo_col.at[1, pl.ds(TAIL, length)], 0, -1),
-        (row_edge.at[1], halo_row.at[0], 1, 0),
-        (row_edge.at[0], halo_row.at[1], -1, 0),
+        (nodes.at[length - 1], halo_row.at[0], 1, 0),
+        (nodes.at[0], halo_row.at[1], -1, 0),
         (col_edge.at[1, low], halo_col.at[0, top], 1, 1),
         (col_edge.at[1, top], halo_col.at[0, pl.ds(TAIL + length, TAIL)], -1, 1),
         (col_edge.at[0, low], halo_col.at[1, top], 1, -1),
         (col_edge.at[0, top], halo_col.at[1, pl.ds(TAIL + length, TAIL)], -1, -1),
     ]
-    halo = [
-        send(src, dst, send_sem.at[i], recv_sem.at[i], dr, dc)
-        for i, (src, dst, dr, dc) in enumerate(plan)
-    ]
-    for copy in stage:
-        copy.wait()
-    mean, power, number = combine([stats[...]] + [first[k] for k in range(num_cols - 1)])
-    latent = stats.shape[1]
-    middle[...] = jnp.concatenate([mean, power, number, jnp.zeros((5, latent), F32)], axis=0)
-    base = num_cols - 1
-    stage = [
-        send(middle, second.at[k - 1], stat_send.at[base + k - 1], stat_recv.at[base + k - 1], k, 0)
-        for k in range(1, num_rows)
-    ]
-    for copy in stage:
-        copy.wait()
-    mean, power, number = combine([middle[...]] + [second[k] for k in range(num_rows - 1)])
-    spread = lax.rsqrt(power / number + EPS)
-    norm[...] = jnp.concatenate([mean, spread, jnp.zeros((6, latent), F32)], axis=0)
-    for copy in halo:
-        copy.wait()
+
+    def halo():
+        return [
+            copy_of(src, dst, send_sem.at[i], recv_sem.at[i], dr, dc)
+            for i, (src, dst, dr, dc) in enumerate(plan)
+        ]
+
+    @pl.when(step == 0)
+    def _():
+        for dr, dc in peers:
+            pl.semaphore_signal(barrier, inc=1, device_id=at(dr, dc), device_id_type=MESH)
+        shift[...] = jnp.broadcast_to(edges[0, 0:TAIL, :].astype(F32)[0:1], shift.shape)
+        acc_sum[...] = jnp.zeros_like(acc_sum)
+        acc_sq[...] = jnp.zeros_like(acc_sq)
+        flat = nodes[...].reshape(length * cols, latent)
+        line = lax.broadcasted_iota(jnp.int32, (length, length * cols), 0) * cols
+        place = lax.broadcasted_iota(jnp.int32, (length, length * cols), 1)
+        for side, offset in enumerate((0, cols - 1)):
+            pick = jnp.where(place == line + offset, 1.0, 0.0).astype(BF16)
+            col_edge[side] = dot(pick, flat).astype(BF16)
+
+    @pl.when(step == steps // 2)
+    def _():
+        pl.semaphore_wait(barrier, len(peers))
+        for copy in halo():
+            copy.start()
+
+    base = shift[0:1, :]
+    total, square = acc_sum[...], acc_sq[...]
+    group = 64
+    for k in range(bands_step):
+        count = counts[step * bands_step + k]
+        for lo in range(0, slots, group):
+            moved = edges[k, lo : lo + group, :].astype(F32) - base
+            if lo + group > slots // 2:
+                rows = lax.broadcasted_iota(jnp.int32, (group, latent), 0) + lo
+                moved = jnp.where(rows < count, moved, 0.0)
+            total += jnp.sum(moved.reshape(-1, 8, latent), axis=0)
+            square += jnp.sum((moved * moved).reshape(-1, 8, latent), axis=0)
+    acc_sum[...] = total
+    acc_sq[...] = square
+
+    @pl.when(step == steps - 1)
+    def _():
+        amount = counts[0]
+        for k in range(1, counts.shape[0]):
+            amount = amount + counts[k]
+        amount = jnp.full((1, latent), amount.astype(F32))
+        offset = jnp.sum(acc_sum[...], axis=0, keepdims=True) / amount
+        spare = jnp.sum(acc_sq[...], axis=0, keepdims=True) - offset * offset * amount
+        stats[...] = jnp.concatenate([base + offset, spare, amount], axis=1)
+        stage = [
+            copy_of(stats, first.at[k - 1], stat_send.at[k - 1], stat_recv.at[k - 1], 0, k)
+            for k in range(1, num_cols)
+        ]
+        for copy in stage:
+            copy.start()
+        for copy in stage:
+            copy.wait()
+        merged = combine([stats[...]] + [first[k] for k in range(num_cols - 1)], latent)
+        middle[...] = jnp.concatenate(merged, axis=1)
+        past = num_cols - 1
+        stage = [
+            copy_of(
+                middle, second.at[k - 1], stat_send.at[past + k - 1],
+                stat_recv.at[past + k - 1], k, 0,
+            )
+            for k in range(1, num_rows)
+        ]
+        for copy in stage:
+            copy.start()
+        for copy in halo():
+            copy.wait()
+        row_out[...] = halo_row[...]
+        col_out[...] = halo_col[...]
+        for copy in stage:
+            copy.wait()
+        mean, power, number = combine(
+            [middle[...]] + [second[k] for k in range(num_rows - 1)], latent
+        )
+        spread = lax.rsqrt(jnp.maximum(power / number, 0.0) + EPS)
+        norm[...] = jnp.concatenate([mean, spread, jnp.zeros((6, latent), F32)], axis=0)
 
 
 def twice(w):
@@ -262,22 +282,11 @@
     flat = nodes.reshape(rows * cols, latent)
 
     step = 2 if bands % 2 == 0 else 1
-    stats = pl.pallas_call(
-        functools.partial(stats_kernel, step),
-        grid=(bands // step,),
-        in_specs=[SMEM, pl.BlockSpec((step, slots, latent), lambda i: (i, 0, 0))],
-        out_specs=VMEM,
-        out_shape=jax.ShapeDtypeStruct((8, latent), F32),
-        scratch_shapes=[pltpu.VMEM((8, latent), F32)] * 3,
-        name="stats",
-    )(tile_counts, tile_edges)
-
-    row_edge = jnp.stack([nodes[0], nodes[-1]])
-    col_edge = jnp.stack([nodes[:, 0], nodes[:, -1]])
     stages = num_cols + num_rows - 2
     norm, halo_row, halo_col = pl.pallas_call(
-        functools.partial(exchange_kernel, num_rows, num_cols),
-        in_specs=[VMEM] * 3,
+        functools.partial(exchange_kernel, num_rows, num_cols, step),
+        grid=(bands // step,),
+        in_specs=[SMEM, pl.BlockSpec((step, slots, latent), lambda i: (i, 0, 0)), VMEM],
         out_specs=[VMEM] * 3,
         out_shape=[
             jax.ShapeDtypeStruct((8, latent), F32),
@@ -285,9 +294,16 @@
             jax.ShapeDtypeStruct((2, rows + 2 * TAIL, latent), BF16),
         ],
         scratch_shapes=[
-            pltpu.VMEM((max(num_cols - 1, 1), 8, latent), F32),
+            pltpu.VMEM((2, cols, latent), BF16),
+            pltpu.VMEM((2, rows + 2 * TAIL, latent), BF16),
             pltpu.VMEM((8, latent), F32),
-            pltpu.VMEM((max(num_rows - 1, 1), 8, latent), F32),
+            pltpu.VMEM((8, latent), F32),
+            pltpu.VMEM((8, latent), F32),
+            pltpu.VMEM((2, rows, latent), BF16),
+            pltpu.VMEM((1, 3 * latent), F32),
+            pltpu.VMEM((max(num_cols - 1, 1), 1, 3 * latent), F32),
+            pltpu.VMEM((1, 3 * latent), F32),
+            pltpu.VMEM((max(num_rows - 1, 1), 1, 3 * latent), F32),
             pltpu.SemaphoreType.DMA((8,)),
             pltpu.SemaphoreType.DMA((8,)),
             pltpu.SemaphoreType.DMA((stages,)),
@@ -295,7 +311,7 @@
         ],
         compiler_params=pltpu.CompilerParams(collective_id=0, has_side_effects=True),
         name="exchange",
-    )(stats, row_edge, col_edge)
+    )(tile_counts, tile_edges, nodes)
 
     band_nodes = band_rows * cols
     table = round_up((band_rows + 2) * cols + 16, 128)

time: 48 us -> 43 us (0.90)
  Pallas kernels: 44 us -> 42.1 us
  local copies, waits for them, and re-layouts: 1.75 us -> 0 us
  other arithmetic: 1.23 us -> 0 us
    pallas_call x2 -> x1, Pallas kernels: 19.9 us -> 18 us  [per_device(): pl.pallas_call(functools.partial(exchange_kernel, num_rows, num_cols, ste...]
    slice x2 -> x0, local copies, waits for them, and re-layouts: 1.74 us -> none  [the longest x1 1.03 us: per_device(): col_edge = jnp.stack([nodes[:, 0], nodes[:, -1]])]
    another operation x2 -> x0, other arithmetic: 1.23 us -> none  [the longest x1 0.62 us: per_device(): col_edge = jnp.stack([nodes[:, 0], nodes[:, -1]])]
where the time goes in v2:
time: 43 us; the launch traced here: 42.8 us
  Pallas kernels  42.1 us (98%)
  between operations  0.64 us (1%)
    pallas_call x1, Pallas kernels, per_device(): pl.pallas_call(functools.partial(main_kernel, band_rows, cols), grid=(ban...  24.1 us
    pallas_call x1, Pallas kernels, per_device(): pl.pallas_call(functools.partial(exchange_kernel, num_rows, num_cols, ste...  18 us

profile of v2, /device:TPU:0, one launch (start us, length us, event | category | flops | bytes accessed | tf_op | source)
XLA Modules:
  0.0 42.8 jit_solution(16791000448698579250)
XLA Ops:
  0.6 18.0 %exchange.1 = (f32[8,128]{1,0:T(8,128)}, bf16[2,32,128]{2,1,0:T(8,128)(2,1)}, bf16[2,96,128]{2,1,0:T(8,128)(2,1)}) custom-call(s32[16]{0:T(128)} %bitcast.16, bf16[16,1024,128]{2,1,0:T(8,128)(2,1)} %bitcast.11, bf16[64,32,128]{2,1,0:T(8,128)(2,1)} %nodes.1), custom_call_target="tpu_custom_call" | custom-call | tf_op jit(solution)/shard_map/exchange/pallas_call | solution.py:286
  18.7 24.1 %processor.1 = (bf16[16,1024,128]{2,1,0:T(8,128)(2,1)}, bf16[2048,128]{1,0:T(8,128)(2,1)}) custom-call(s32[16]{0:T(128)} %bitcast.17, bf16[16,1024,128]{2,1,0:T(8,128)(2,1)} %bitcast.12, s32[16,1024]{1,0:T(8,128)} %bitcast.14, s32[16,1024]{1,0:T(8,128)} %bitcast.15, bf16[2048,128]{1,0:T(8,128)(2,1)} %bitcast.13, ...), custom_call_target="tpu_custom_call" | custom-call | tf_op jit(solution)/shard_map/processor/pallas_call | solution.py:318

commit v3 on v2

--- a/solution.py
+++ b/solution.py
@@ -14,7 +14,6 @@
 BF16 = jnp.bfloat16
 VMEM = pl.BlockSpec(memory_space=pltpu.VMEM)
 SMEM = pl.BlockSpec(memory_space=pltpu.SMEM)
-ANY = pl.BlockSpec(memory_space=pl.ANY)
 
 
 def dot(a, b):
@@ -83,12 +82,6 @@
         for side, offset in enumerate((0, cols - 1)):
             pick = jnp.where(place == line + offset, 1.0, 0.0).astype(BF16)
             col_edge[side] = dot(pick, flat).astype(BF16)
-
-    @pl.when(step == steps // 2)
-    def _():
-        pl.semaphore_wait(barrier, len(peers))
-        for copy in halo():
-            copy.start()
 
     base = shift[0:1, :]
     total, square = acc_sum[...], acc_sq[...]
@@ -118,7 +111,10 @@
             copy_of(stats, first.at[k - 1], stat_send.at[k - 1], stat_recv.at[k - 1], 0, k)
             for k in range(1, num_cols)
         ]
+        pl.semaphore_wait(barrier, len(peers))
         for copy in stage:
+            copy.start()
+        for copy in halo():
             copy.start()
         for copy in stage:
             copy.wait()
@@ -160,20 +156,114 @@
 
 
 def main_kernel(
-    band_rows, cols, counts, edges, send_all, recv_all, nodes, halo_row, halo_col, norm,
+    band_rows, cols, chunks, even_last, counts, edges, send_all, recv_all, nodes, halo_row, halo_col, norm,
     w_in, w_hid, w_out, bias, gain, shift, v_in, v_hid, v_out, n_bias, n_gain, n_shift,
     new_edges, new_nodes,
     proj_send, proj_left, proj_right, proj_recv, mixed, two_hid, two_out, two_mean, gathered,
+    one_even, norm_even, one_odd, norm_odd,
 ):
-    band = pl.program_id(0)
+    step, bands = pl.program_id(0), pl.num_programs(0) - 1
     slots, latent = edges.shape[1:]
     band_nodes = band_rows * cols
     window_rows = band_rows + 2
     main = window_rows * cols
     table = mixed.shape[0] - band_nodes - latent
     half = slots // 2
-
-    @pl.when(band == 0)
+    length = half // chunks
+    even, odd = (one_even, norm_even), (one_odd, norm_odd)
+
+    def spread_rows(index, lo):
+        return jnp.broadcast_to(index[:, lo : lo + 128], (128, 128)).T
+
+    def pick(values, width, offset=0):
+        lanes = lax.broadcasted_iota(jnp.int32, (values.shape[0], width), 1) + offset
+        return jnp.where(values == lanes, 1.0, 0.0).astype(BF16)
+
+    def head(store):
+        one, normed = store
+        band = step
+        start = pl.multiple_of(band * band_nodes, band_nodes)
+        side = TAIL - 1 + band * band_rows
+        mixed[0:main, :] = proj_send[pl.ds(start, main), :]
+        mixed[main : main + 16, :] = jnp.concatenate(
+            [proj_left[pl.ds(side, 8), :], proj_right[pl.ds(side, 8), :]], axis=0
+        ).astype(BF16)
+        mixed[table : table + band_nodes, :] = proj_recv[pl.ds(start, band_nodes), :]
+        weights = mixed[...]
+        send = send_all[pl.ds(band, 1), :]
+        recv = recv_all[pl.ds(band, 1), :]
+        row = sum((send >= (cols + 2) * k).astype(jnp.int32) for k in range(1, window_rows))
+        col = send - (cols + 2) * row
+        place = jnp.where(
+            col == 0, main + row, jnp.where(col == cols + 1, main + 8 + row, row * cols + col - 1)
+        )
+        mean, spread = norm[0:1, :], norm[1:2, :]
+
+        def run(chunk):
+            pieces = []
+            for part in range(2):
+                first = part * half + chunk * length
+                for lo in range(first, first + length, 128):
+                    s, q = spread_rows(place, lo), spread_rows(recv, lo)
+                    hot = [pick(s, 128, off) for off in range(0, table, 128)]
+                    hot += [pick(q, 128, off) for off in range(0, band_nodes, 128)]
+                    block = edges[0, lo : lo + 128, :].astype(F32)
+                    value = ((block - mean) * spread).astype(BF16)
+                    normed[lo : lo + 128, :] = value
+                    pieces.append(jnp.concatenate(hot + [value], axis=1))
+            result = dot(jnp.concatenate(pieces, axis=0), weights)
+            result = jnp.maximum(result, 0.0).astype(BF16)
+            lines = slice(chunk * length, (chunk + 1) * length)
+            one[lines, :] = jnp.concatenate([result[:length], result[length:]], axis=1)
+
+        return run
+
+    def tail(store):
+        one, normed = store
+        band = step - 1
+        start = pl.multiple_of(band * band_nodes, band_nodes)
+        recv = recv_all[pl.ds(band, 1), :]
+        count = counts[band]
+        bias_hid = jnp.concatenate([bias[1:2, :]] * 2, axis=1)
+        bias_msg = bias[2:3, :] - jnp.mean(bias[2:3, :], axis=-1, keepdims=True)
+        bias_out = jnp.concatenate([bias_msg] * 2, axis=1)
+        sums = []
+
+        def run(chunk):
+            lines = slice(chunk * length, (chunk + 1) * length)
+            two = jnp.maximum(dot(one[lines, :], two_hid[...]) + bias_hid, 0.0).astype(BF16)
+            message = dot(two, two_out[...]) + bias_out
+            power = dot((message * message).astype(BF16), two_mean[...])
+            unit = message * lax.rsqrt(power + EPS)
+            fresh, picks = [], []
+            for part in range(2):
+                lo = part * half + chunk * length
+                value = normed[lo : lo + length, :].astype(F32) + shift[...]
+                value = value + unit[:, part * latent : (part + 1) * latent] * gain[...]
+                if lo + length > slots // 2:
+                    rows = lax.broadcasted_iota(jnp.int32, (length, latent), 0) + lo
+                    value = jnp.where(rows < count, value, 0.0)
+                value = value.astype(BF16)
+                new_edges[0, lo : lo + length, :] = value
+                fresh.append(value)
+                places = lax.broadcasted_iota(jnp.int32, (band_nodes, length), 0)
+                hit = places == recv[:, lo : lo + length]
+                picks.append(jnp.where(hit, 1.0, 0.0).astype(BF16))
+            fresh, picks = jnp.concatenate(fresh, axis=0), jnp.concatenate(picks, axis=1)
+            sums.append(dot(picks, fresh))
+            if chunk == chunks - 1:
+                gathered[pl.ds(start, band_nodes), :] = sum(sums).astype(BF16)
+
+        return run
+
+    def work(before, after):
+        runs = [tail(before)] if before else []
+        runs += [head(after)] if after else []
+        for chunk in range(chunks):
+            for run in runs:
+                run(chunk)
+
+    @pl.when(step == 0)
     def _():
         w_send = w_in[latent : 2 * latent, :]
         w_recv = w_in[2 * latent :, :]
@@ -189,78 +279,43 @@
         two_hid[...] = twice(w_hid[...])
         two_out[...] = twice(centred(w_out[...]).astype(BF16))
         two_mean[...] = twice(jnp.full((latent, latent), 1.0 / latent, BF16))
-
-    start = pl.multiple_of(band * band_nodes, band_nodes)
-    side = TAIL - 1 + band * band_rows
-    mixed[0:main, :] = proj_send[pl.ds(start, main), :]
-    mixed[main : main + 16, :] = jnp.concatenate(
-        [proj_left[pl.ds(side, 8), :], proj_right[pl.ds(side, 8), :]], axis=0
-    ).astype(BF16)
-    mixed[table : table + band_nodes, :] = proj_recv[pl.ds(start, band_nodes), :]
-    weights = mixed[...]
-
-    send = send_all[pl.ds(band, 1), :]
-    recv = recv_all[pl.ds(band, 1), :]
-    row = sum((send >= (cols + 2) * k).astype(jnp.int32) for k in range(1, window_rows))
-    col = send - (cols + 2) * row
-    place = jnp.where(
-        col == 0, main + row, jnp.where(col == cols + 1, main + 8 + row, row * cols + col - 1)
-    )
-    count = counts[band]
-    mean, spread = norm[0:1, :], norm[1:2, :]
-    bias_hid = jnp.concatenate([bias[1:2, :]] * 2, axis=1)
-    bias_msg = bias[2:3, :] - jnp.mean(bias[2:3, :], axis=-1, keepdims=True)
-    bias_out = jnp.concatenate([bias_msg] * 2, axis=1)
-
-    def spread_rows(index, lo):
-        return jnp.broadcast_to(index[:, lo : lo + 128], (128, 128)).T
-
-    def pick(values, width, offset=0):
-        lanes = lax.broadcasted_iota(jnp.int32, (values.shape[0], width), 1) + offset
-        return jnp.where(values == lanes, 1.0, 0.0).astype(BF16)
-
-    ones, normed = [], []
-    for part in range(2):
-        pieces = []
-        for lo in range(part * half, (part + 1) * half, 128):
-            s, q = spread_rows(place, lo), spread_rows(recv, lo)
-            hot = [pick(s, 128, off) for off in range(0, table, 128)]
-            hot += [pick(q, 128, off) for off in range(0, band_nodes, 128)]
-            pieces.append(jnp.concatenate(hot, axis=1))
-        hot = jnp.concatenate(pieces, axis=0)
-        block = edges[0, part * half : (part + 1) * half, :].astype(F32)
-        value = ((block - mean) * spread).astype(BF16)
-        normed.append(value)
-        joined = jnp.concatenate([hot, value], axis=1)
-        ones.append(jnp.maximum(dot(joined, weights), 0.0).astype(BF16))
-    one = jnp.concatenate(ones, axis=1)
-    two = jnp.maximum(dot(one, two_hid[...]) + bias_hid, 0.0).astype(BF16)
-    message = dot(two, two_out[...]) + bias_out
-    power = dot((message * message).astype(BF16), two_mean[...])
-    unit = message * lax.rsqrt(power + EPS)
-    fresh = []
-    for part in range(2):
-        rows = lax.broadcasted_iota(jnp.int32, (half, latent), 0) + part * half
-        value = normed[part].astype(F32) + unit[:, part * latent : (part + 1) * latent] * gain[...] + shift[...]
-        value = jnp.where(rows < count, value, 0.0).astype(BF16)
-        new_edges[0, part * half : (part + 1) * half, :] = value
-        fresh.append(value)
-    fresh = jnp.concatenate(fresh, axis=0)
-    places = lax.broadcasted_iota(jnp.int32, (band_nodes, slots), 0)
-    pick_recv = jnp.where(places == recv, 1.0, 0.0).astype(BF16)
-    gathered[pl.ds(start, band_nodes), :] = dot(pick_recv, fresh).astype(BF16)
-
-    @pl.when(band == pl.num_programs(0) - 1)
-    def _():
+        work(None, even)
+
+    inside = (step > 0) & (step < bands)
+
+    @pl.when(inside & (step % 2 == 1))
+    def _():
+        work(even, odd)
+
+    @pl.when(inside & (step % 2 == 0))
+    def _():
+        work(odd, even)
+
+    @pl.when(step == bands)
+    def _():
+        work(even if even_last else odd, None)
         own = nodes[...]
+        middle = own.shape[0] // 2
+
+        def pair(value):
+            return jnp.concatenate([value[:middle], value[middle:]], axis=1)
+
+        def wide(row):
+            return jnp.concatenate([row, row], axis=1)
+
         joined = jnp.concatenate([own, gathered[...]], axis=1)
         node_one = jnp.maximum(dot(joined, v_in[...]) + n_bias[0:1, :], 0.0).astype(BF16)
-        node_two = jnp.maximum(dot(node_one, v_hid[...]) + n_bias[1:2, :], 0.0).astype(BF16)
+        node_two = dot(pair(node_one), twice(v_hid[...])) + wide(n_bias[1:2, :])
+        node_two = jnp.maximum(node_two, 0.0).astype(BF16)
         out_bias = n_bias[2:3, :] - jnp.mean(n_bias[2:3, :], axis=-1, keepdims=True)
-        note = dot(node_two, centred(v_out[...]).astype(BF16)) + out_bias
-        level = dot((note * note).astype(BF16), jnp.full((latent, latent), 1.0 / latent, BF16))
-        value = own.astype(F32) + note * lax.rsqrt(level + EPS) * n_gain[...] + n_shift[...]
-        new_nodes[...] = value.astype(BF16)
+        note = dot(node_two, twice(centred(v_out[...]).astype(BF16))) + wide(out_bias)
+        level = dot((note * note).astype(BF16), two_mean[...])
+        unit = note * lax.rsqrt(level + EPS)
+        for part in range(2):
+            rows = slice(part * middle, (part + 1) * middle)
+            value = own[rows].astype(F32) + n_shift[...]
+            value = value + unit[:, part * latent : (part + 1) * latent] * n_gain[...]
+            new_nodes[rows, :] = value.astype(BF16)
 
 
 def round_up(value, unit):
@@ -316,10 +371,15 @@
     band_nodes = band_rows * cols
     table = round_up((band_rows + 2) * cols + 16, 128)
     out_edges, out_nodes = pl.pallas_call(
-        functools.partial(main_kernel, band_rows, cols),
-        grid=(bands,),
-        in_specs=[SMEM, pl.BlockSpec((1, slots, latent), lambda i: (i, 0, 0))] + [VMEM] * 18,
-        out_specs=[pl.BlockSpec((1, slots, latent), lambda i: (i, 0, 0)), VMEM],
+        functools.partial(main_kernel, band_rows, cols, 1, bands % 2 == 1),
+        grid=(bands + 1,),
+        in_specs=[
+            SMEM,
+            pl.BlockSpec((1, slots, latent), lambda i: (jnp.minimum(i, bands - 1), 0, 0)),
+        ] + [VMEM] * 18,
+        out_specs=[
+            pl.BlockSpec((1, slots, latent), lambda i: (jnp.maximum(i - 1, 0), 0, 0)), VMEM,
+        ],
         out_shape=[
             jax.ShapeDtypeStruct((bands, slots, latent), BF16),
             jax.ShapeDtypeStruct((rows * cols, latent), BF16),
@@ -334,7 +394,10 @@
             pltpu.VMEM((2 * latent, 2 * latent), BF16),
             pltpu.VMEM((2 * latent, 2 * latent), BF16),
             pltpu.VMEM((rows * cols, latent), BF16),
-        ],
+        ] + [
+            pltpu.VMEM((slots // 2, 2 * latent), BF16),
+            pltpu.VMEM((slots, latent), BF16),
+        ] * 2,
         name="processor",
     )(
         tile_counts, tile_edges, tile_send, tile_recv, flat, halo_row, halo_col, norm,

time: 43 us -> 42.2 us (0.981)
  Pallas kernels: 42.1 us -> 41.3 us
    pallas_call x1, Pallas kernels: 24.1 us -> 23.3 us  [per_device(): pl.pallas_call(functools.partial(main_kernel, band_rows, cols, 1, bands %...]
where the time goes in v3:
time: 42.2 us; the launch traced here: 41.9 us
  Pallas kernels  41.3 us (98%)
  between operations  0.64 us (2%)
    pallas_call x1, Pallas kernels, per_device(): pl.pallas_call(functools.partial(main_kernel, band_rows, cols, 1, bands %...  23.3 us
    pallas_call x1, Pallas kernels, per_device(): pl.pallas_call(functools.partial(exchange_kernel, num_rows, num_cols, ste...  18 us

profile of v3, /device:TPU:0, one launch (start us, length us, event | category | flops | bytes accessed | tf_op | source)
XLA Modules:
  0.0 41.9 jit_solution(3872972351084624866)
XLA Ops:
  0.6 18.0 %exchange.1 = (f32[8,128]{1,0:T(8,128)}, bf16[2,32,128]{2,1,0:T(8,128)(2,1)}, bf16[2,96,128]{2,1,0:T(8,128)(2,1)}) custom-call(s32[16]{0:T(128)} %bitcast.16, bf16[16,1024,128]{2,1,0:T(8,128)(2,1)} %bitcast.11, bf16[64,32,128]{2,1,0:T(8,128)(2,1)} %nodes.1), custom_call_target="tpu_custom_call" | custom-call | tf_op jit(solution)/shard_map/exchange/pallas_call | solution.py:341
  18.7 23.3 %processor.1 = (bf16[16,1024,128]{2,1,0:T(8,128)(2,1)}, bf16[2048,128]{1,0:T(8,128)(2,1)}) custom-call(s32[16]{0:T(128)} %bitcast.17, bf16[16,1024,128]{2,1,0:T(8,128)(2,1)} %bitcast.12, s32[16,1024]{1,0:T(8,128)} %bitcast.14, s32[16,1024]{1,0:T(8,128)} %bitcast.15, bf16[2048,128]{1,0:T(8,128)(2,1)} %bitcast.13, ...), custom_call_target="tpu_custom_call" | custom-call | tf_op jit(solution)/shard_map/processor/pallas_call | solution.py:373
